TPU v7x, 8 devices: a whole 2x2x1 slice. The times are simulated.
8 devices in a mesh: part: 1 (over z), data: 2 (over y), stage: 4 (over x, core).
Axes of the slice: x: 2, y: 2, z: 1, core: 2. Of those that a mesh axis runs over, the one named last changes fastest.
Arguments:
- x_in: bfloat16 [32, 128, 2048], P(('part', 'data'))
- y_tgt: bfloat16 [32, 128, 2048], P(('part', 'data'))
- w_up: bfloat16 [4, 2048, 5632], P('stage')
- w_down: bfloat16 [4, 5632, 2048], P('stage')
- gain: float32 [4, 2048], P('stage')
Outputs:
- output 1: float32 [4, 2048, 5632], P(('part', 'stage'))
- output 2: float32 [4, 5632, 2048], P(('part', 'stage'))
- output 3: float32 [4, 2048], P(('part', 'stage'))
- output 4: float32 [1], P('part')
All inputs are finite; a program needn't handle non-finite values.
Results may differ from a plain program's by a relative error of at most 0.00258878.
Values are sent between devices in bfloat16 or wider.
A program may use at most 1 GiB of HBM per device.

v0:
```python
import functools

import jax
import jax.numpy as jnp
from jax import lax
from jax.experimental import pallas as pl
from jax.experimental.pallas import tpu as pltpu
from jax.sharding import PartitionSpec as P

MESH = pl.DeviceIdType.MESH
EPS = 1e-6
C0 = 0.7978845608028654
C1 = 0.044715
ROWS = 256
HALF = ROWS // 2
TILE = 512
FWD, BWD, AUX, PRE = 0, 1, 2, 3
NONE = 64 * 17
LAST_DIMS = (((1,), (1,)), ((), ()))
ROW_DIMS = (((0,), (0,)), ((), ()))
F32 = jnp.float32
BF16 = jnp.bfloat16

ORDERS = (
    (
        "P0~", "P1", "P2", "P3", "F2", "F3", "F4", "F5", "F6",
        "F7", "F8", "B0~", "B1~", "B2~", "A0", "A1", "A2~", "B3",
        "B4", "A3", "A4", "B5", "B6", "A5", "A6", "B7", "B8",
    ),
    (
        "P0~", "P1~", "P2", "P3", "F2~", "F3~", "F4~", "F5", "B0",
        "F6", "F7", "B1", "B2~", "A0", "F8", "B3", "B4~", "A1",
        "A2", "B5", "B6~", "A3", "A4", "B7~", "B8", "A5", "A6",
    ),
    (
        "P0~", "P1~", "P2~", "P3~", "B0~", "F2", "F3", "B1", "F4",
        "B2", "F5", "B3", "F6", "B4", "F7", "B5", "F8", "B6",
        "A0", "A1", "B7", "B8", "A2", "A3", "A4", "A5", "A6",
    ),
    (
        "P0~", "P1~", "B0", "P2", "P3", "B1", "F2~", "B2", "F3",
        "B3", "F4", "B4", "F5", "B5", "F6", "B6", "F7", "B7",
        "F8", "B8", "A0", "A1", "A2", "A3", "A4", "A5", "A6",
    ),
)
N_CHAIN = 9
N_OWN = 8
N_EXCH = 7
N_PRE = 2


def gelu_and_grad(pre):
    sq = pre * pre
    th = jnp.tanh(pre * (C0 + (C0 * C1) * sq))
    cdf = 0.5 + 0.5 * th
    grad = cdf + (pre * (C0 + (3.0 * C0 * C1) * sq)) * (cdf * (1.0 - th))
    return pre * cdf, grad


def chain_kernel(orders, tok_total, x_in, y_tgt, w_up, w_down, gain, r_all, u_all, da_all, dh_all, gp_all, x_land, y_land,
                 dg_out, loss_out, w1, w2, main, rb, gp, ub, ring, dgp, dgr, lossacc, lossred, lossbuf,
                 w_ld, main_ld, rb_ld, r_sem, gp_o, gp_i, u_sem, dh_o, x_rcv, dh_rcv, rr_rcv, dd_rcv, y_rcv, dg_rcv, loss_rcv,
                 slot_snd, rr_snd, dd_snd, red_snd, dg_snd, loss_snd):
    n_items = len(orders[0])
    ff, d = w_down.shape
    me_y = lax.axis_index("data")
    sid = lax.axis_index("stage")
    other = 1 - me_y
    first, last = sid == 0, sid == 3
    f_tiles, d_tiles = ff // TILE, d // TILE
    cols = lambda k: pl.ds(k * TILE, TILE)

    def rows_of(chunk):
        return pl.ds(pl.multiple_of(chunk * ROWS, ROWS), ROWS)

    def own_chunk(idx):
        return jnp.where(idx < N_OWN, me_y * N_OWN + idx, other * N_OWN + idx - (N_CHAIN - N_OWN))

    def decode(step):
        code = jnp.int32(NONE)
        for stage_k, seq in enumerate(orders):
            val = jnp.int32(NONE)
            for step_k, item in enumerate(seq):
                val = jnp.where(step == step_k, item, val)
            code = jnp.where(sid == stage_k, val, code)
        return code

    def fields(code):
        kind, idx = lax.rem(code, 4), lax.rem(code // 4, 16)
        return jnp.where(code >= NONE, -1, kind), idx, lax.rem(code // 64, 2) == 1

    def local(src, dst, sem):
        return pltpu.make_async_copy(src, dst, sem)

    def remote(src, dst, snd, rcv, **to):
        return pltpu.make_async_remote_copy(src, dst, snd, rcv, device_id=to, device_id_type=MESH)

    def relay_r(k):
        rows = rows_of(me_y * N_OWN + k)
        return remote(r_all.at[rows, :], r_all.at[rows, :], rr_snd.at[k], rr_rcv.at[k], data=other)

    def relay_dh(k):
        rows = rows_of(me_y * N_OWN + k)
        return remote(dh_all.at[rows, :], dh_all.at[rows, :], dd_snd.at[k], dd_rcv.at[k], data=other)

    def u_out(which, rows):
        dst = u_all if which == 0 else da_all
        return local(ub.at[which], dst.at[rows, :], u_sem.at[which])

    def sends(code):
        kind = fields(code)[0]
        return (((kind == FWD) | (kind == PRE)) & (sid < 3)) | ((kind == BWD) & (sid > 0))

    def wait_slot_send(code, slot):
        pre = fields(code)[0] == PRE

        @pl.when(sends(code) & pre)
        def _():
            half = pl.ds(0, HALF)
            remote(main.at[slot, half, :], x_land.at[half, :], slot_snd.at[slot], x_rcv.at[0], data=other).wait_send()

        @pl.when(sends(code) & jnp.logical_not(pre))
        def _():
            remote(main.at[slot], x_land.at[pl.ds(0, ROWS), :], slot_snd.at[slot], x_rcv.at[0], data=other).wait_send()

    def load_x(idx, dst, sem):
        @pl.when(first & (idx < N_OWN))
        def _():
            local(x_in.at[rows_of(jnp.minimum(idx, N_OWN - 1)), :], dst, sem).start()

        @pl.when(jnp.logical_not(first & (idx < N_OWN)))
        def _():
            local(x_land.at[rows_of(idx), :], dst, sem).start()

    def prefetch(code, step, before, waited=None):
        kind, idx, _ = fields(code)
        slot = lax.rem(step, 3)

        if waited is None:
            wait_slot_send(before, slot)
        else:
            @pl.when(jnp.logical_not(waited))
            def _():
                wait_slot_send(before, slot)

        @pl.when(kind == PRE)
        def _():
            half = pl.ds(pl.multiple_of(idx * HALF, HALF), HALF)
            dst = main.at[slot, in_chunk(idx), :]

            @pl.when(first & (step > 0))
            def _():
                local(x_in.at[half, :], dst, main_ld.at[slot]).start()

            @pl.when(jnp.logical_not(first))
            def _():
                local(x_land.at[half, :], x_land.at[half, :], x_rcv.at[pre_sem(idx)]).wait()
                local(x_land.at[half, :], dst, main_ld.at[slot]).start()

        @pl.when(kind == FWD)
        def _():
            @pl.when(jnp.logical_not(first & (idx < N_OWN)))
            def _():
                local(x_land.at[rows_of(idx), :], x_land.at[rows_of(idx), :], x_rcv.at[idx]).wait()

            load_x(idx, main.at[slot], main_ld.at[slot])

        @pl.when((kind == BWD) & jnp.logical_not(last))
        def _():
            rows = rows_of(own_chunk(idx))
            local(dh_all.at[rows, :], dh_all.at[rows, :], dh_rcv.at[idx]).wait()
            local(dh_all.at[rows, :], main.at[slot], main_ld.at[slot]).start()

            @pl.when(idx < N_EXCH)
            def _():
                relay_dh(idx).start()

        @pl.when(kind == AUX)
        def _():
            rows = rows_of(other * N_OWN + idx)
            local(r_all.at[rows, :], r_all.at[rows, :], rr_rcv.at[idx]).wait()
            local(r_all.at[rows, :], rb.at[0], rb_ld.at[0]).start()
            local(dh_all.at[rows, :], dh_all.at[rows, :], dd_rcv.at[idx]).wait()
            local(dh_all.at[rows, :], main.at[slot], main_ld.at[slot]).start()

    def pre_sem(idx):
        return jnp.where(lax.rem(idx, 2) == 0, N_CHAIN + idx // 2, idx // 2)

    def in_chunk(idx):
        return pl.ds(pl.multiple_of(lax.rem(idx, 2) * HALF, HALF), HALF)

    def load_gp(code, lo=0, hi=None):
        kind, idx, _ = fields(code)
        lanes = pl.ds(lo, (hi or ff) - lo)

        @pl.when((kind == BWD) & jnp.logical_not(last))
        def _():
            local(gp_all.at[rows_of(idx), lanes], gp.at[:, lanes], gp_i).start()

    def normalise(slot, rws):
        acc = jnp.zeros((rws.size, 128), F32)
        for k in range(d // 128):
            xk = main[slot, rws, pl.ds(k * 128, 128)].astype(F32)
            acc = acc + xk * xk
        q = lax.rsqrt(jnp.sum(acc, axis=-1, keepdims=True) * (1.0 / d) + EPS)
        for k in range(d // 128):
            lanes = pl.ds(k * 128, 128)
            rb[0, rws, lanes] = (main[slot, rws, lanes].astype(F32) * q * gain[:, lanes]).astype(BF16)

    def up_tiles(rws):
        n = rws.size
        for k in range(f_tiles + 1):
            if k > 0:
                act, grad = gelu_and_grad(ring[(k - 1) % 2, pl.ds(0, n), :])
                ub[0, rws, cols(k - 1)] = act.astype(BF16)
                gp[rws, cols(k - 1)] = grad
            if k < f_tiles:
                ring[k % 2, pl.ds(0, n), :] = jnp.dot(rb[0, rws, :], w1[:, cols(k)], preferred_element_type=F32)

    def down_tiles(lo, hi, slot, out_slot, rws, count):
        n = rws.size
        for k in range(lo, hi + 1):
            if k > lo:
                upd = ring[(k - 1) % 2, pl.ds(0, n), :]
                h = (main[slot, rws, cols(k - 1)].astype(F32) + upd).astype(BF16)
                err = h.astype(F32) - rb[1, rws, cols(k - 1)].astype(F32)
                main[out_slot, rws, cols(k - 1)] = jnp.where(last, (err * (1.0 / tok_total)).astype(BF16), h)
                part = jnp.sum((err * err).reshape(n // 8, 8, TILE), axis=0)
                lossacc[:, cols(k - 1)] += jnp.where(count, part, 0.0)
            if k < hi:
                ring[k % 2, pl.ds(0, n), :] = jnp.dot(ub[0, rws, :], w2[:, cols(k)], preferred_element_type=F32)

    @pl.when(first)
    def _():
        half = pl.ds(0, HALF)
        local(x_in.at[half, :], main.at[0, half, :], main_ld.at[0]).start()

    for k in range(2):
        half = pl.ds(k * (d // 2), d // 2)
        local(w_up.at[half, :], w1.at[half, :], w_ld.at[0]).start()
    def load_w2(k):
        lanes = pl.ds(k * (d // 2), d // 2)
        return local(w_down.at[:, lanes], w2.at[:, lanes], w_ld.at[1 + k])

    @pl.when(jnp.logical_not(first))
    def _():
        for k in range(2):
            load_w2(k).start()

    share = pl.ds(N_EXCH * ROWS, ROWS)
    share_x = remote(x_in.at[share, :], x_land.at[pl.ds(N_OWN * ROWS, ROWS), :], red_snd, x_rcv.at[N_OWN], data=other)
    share_y = remote(y_tgt.at[share, :], y_land, red_snd, y_rcv, data=other)

    @pl.when(first)
    def _():
        share_x.start()

    @pl.when(last)
    def _():
        share_y.start()

    dgp[...] = jnp.zeros_like(dgp)
    lossacc[...] = jnp.zeros_like(lossacc)
    for k in range(d // 128):
        rb[1, :, pl.ds(k * 128, 128)] = jnp.zeros((ROWS, 128), BF16)

    d_half = d_tiles // 2

    def send_half(k, slot, rws, land, sem):
        lanes = pl.ds(k * (d // 2), d // 2)

        @pl.when(sid < 3)
        def _():
            remote(main.at[slot, rws, lanes], x_land.at[land, lanes], slot_snd.at[slot], x_rcv.at[sem],
                   stage=jnp.minimum(sid + 1, 3)).start()

    def run_pre(step, idx, slot, nxt, early, before, prev):
        rws, at = in_chunk(idx), pl.ds(pl.multiple_of(idx * HALF, HALF), HALF)
        odd = lax.rem(idx, 2)
        own = pl.ds(pl.multiple_of(me_y * N_OWN * ROWS + idx * HALF, HALF), HALF)

        @pl.when(last)
        def _():
            local(y_tgt.at[at, :], rb.at[1, rws, :], rb_ld.at[1]).start()

        local(x_in.at[pl.ds(0, HALF), :], main.at[slot, rws, :], main_ld.at[slot]).wait()
        for h in range(2):
            normalise(slot, pl.ds(pl.multiple_of(odd * HALF + h * (HALF // 2), HALF // 2), HALF // 2))
        r_out = local(rb.at[0, rws, :], r_all.at[own, :], r_sem)
        r_out.start()

        @pl.when(step == 0)
        def _():
            local(w_up, w1, w_ld.at[0]).wait()

        @pl.when((step == 0) & first)
        def _():
            for k in range(2):
                load_w2(k).start()

        up_tiles(rws)
        r_out.wait()

        @pl.when(odd == 1)
        def _():
            relay_r(idx // 2).start()

        act_out = local(ub.at[0, rws, :], u_all.at[own, :], u_sem.at[0])
        act_out.start()
        gp_out = local(gp.at[rws, :], gp_all.at[at, :], gp_o)

        @pl.when(jnp.logical_not(last))
        def _():
            gp_out.start()

        @pl.when(step == 0)
        def _():
            load_w2(0).wait()

        @pl.when(last)
        def _():
            local(y_tgt.at[at, :], rb.at[1, rws, :], rb_ld.at[1]).wait()

        out_slot = jnp.where(last, lax.rem(step + 2 - odd, 3), slot)

        @pl.when(last & (odd == 0))
        def _():
            wait_slot_send(prev, out_slot)

        down_tiles(0, d_half, slot, out_slot, rws, last)
        send_half(0, slot, rws, at, pre_sem(idx))
        act_out.wait()

        @pl.when(jnp.logical_not(last))
        def _():
            gp_out.wait()

        load_gp(nxt)

        @pl.when(early)
        def _():
            prefetch(nxt, step + 1, before, last & (odd == 1))

        @pl.when(step == 0)
        def _():
            load_w2(1).wait()

        down_tiles(d_half, d_tiles, slot, out_slot, rws, last)
        send_half(1, slot, rws, at, pre_sem(idx))

    def up_phase(step, kind, idx, slot, rows):
        fwd = kind == FWD
        r_out = local(rb.at[0], r_all.at[rows, :], r_sem)
        gp_out = local(gp, gp_all.at[rows_of(idx), :], gp_o)

        @pl.when(fwd & last)
        def _():
            @pl.when(idx < N_OWN)
            def _():
                local(y_tgt.at[rows_of(jnp.minimum(idx, N_OWN - 1)), :], rb.at[1], rb_ld.at[1]).start()

            @pl.when(idx >= N_OWN)
            def _():
                local(y_land, y_land, y_rcv).wait()
                local(y_land, rb.at[1], rb_ld.at[1]).start()

        @pl.when(fwd)
        def _():
            local(x_in.at[pl.ds(0, ROWS), :], main.at[slot], main_ld.at[slot]).wait()
            for h in range(4):
                normalise(slot, pl.ds(h * (ROWS // 4), ROWS // 4))
            r_out.start()

        @pl.when(kind == AUX)
        def _():
            local(r_all.at[pl.ds(0, ROWS), :], rb.at[0], rb_ld.at[0]).wait()

        up_tiles(pl.ds(0, ROWS))
        u_out(0, rows).start()

        @pl.when(fwd)
        def _():
            r_out.wait()

        @pl.when(fwd & (idx < N_EXCH))
        def _():
            relay_r(jnp.minimum(idx, N_EXCH - 1)).start()

        @pl.when(fwd & jnp.logical_not(last))
        def _():
            gp_out.start()

    def down_phase(step, idx, slot, nxt, early, before, after_aux):
        @pl.when(last)
        def _():
            local(y_land, rb.at[1], rb_ld.at[1]).wait()

        out_slot = jnp.where(last, lax.rem(step + 1, 3), slot)
        count = last & (idx < N_OWN)
        every = pl.ds(0, ROWS)
        down_tiles(0, d_half, slot, out_slot, every, count)
        send_half(0, slot, every, rows_of(idx), idx)
        u_out(0, every).wait()

        @pl.when(after_aux)
        def _():
            u_out(1, every).wait()

        @pl.when(jnp.logical_not(last))
        def _():
            local(gp, gp_all.at[every, :], gp_o).wait()

        load_gp(nxt)

        @pl.when(early)
        def _():
            prefetch(nxt, step + 1, before)

        down_tiles(d_half, d_tiles, slot, out_slot, every, count)
        send_half(1, slot, every, rows_of(idx), idx)

    def back_phase(step, kind, idx, slot, rows, nxt, early, before, after_aux):
        bwd, aux = kind == BWD, kind == AUX
        dh_out = local(main.at[slot], dh_all.at[rows, :], dh_o)

        @pl.when(bwd)
        def _():
            load_x(idx, rb.at[1], rb_ld.at[1])

        @pl.when(bwd & last)
        def _():
            dh_out.start()

        @pl.when(aux | jnp.logical_not(last))
        def _():
            local(x_in.at[pl.ds(0, ROWS), :], main.at[slot], main_ld.at[slot]).wait()

        @pl.when(bwd & jnp.logical_not(last))
        def _():
            local(gp_all.at[pl.ds(0, ROWS), :], gp, gp_i).wait()

        @pl.when(after_aux)
        def _():
            u_out(1, rows).wait()

        @pl.when(aux & early)
        def _():
            prefetch(nxt, step + 1, before)

        for k in range(f_tiles):
            du = lax.dot_general(main[slot], w2[cols(k), :], LAST_DIMS, preferred_element_type=F32)
            ub[1, :, cols(k)] = (du * gp[:, cols(k)]).astype(BF16)
        u_out(1, rows).start()

        @pl.when(aux)
        def _():
            u_out(0, rows).wait()
            load_gp(nxt)

        @pl.when(bwd & last)
        def _():
            dh_out.wait()

        @pl.when(bwd & last & (idx < N_EXCH))
        def _():
            relay_dh(jnp.minimum(idx, N_EXCH - 1)).start()

    def grad_phase(step, idx, slot, rows, nxt, early, before):
        local(x_land.at[pl.ds(0, ROWS), :], rb.at[1], rb_ld.at[1]).wait()

        def r_done(k):
            sq = jnp.zeros((ROWS, 128), F32)
            pr = jnp.zeros((ROWS, 128), F32)
            for j in range(TILE // 128):
                lanes = pl.ds(k * TILE + j * 128, 128)
                xk = rb[1, :, lanes].astype(F32)
                sq = sq + xk * xk
                pr = pr + gp[:, lanes] * gain[:, lanes] * xk
            sums = (pl.ds(0, ROWS), pl.ds(0, 128))
            ring[0, *sums] = sq if k == 0 else ring[0, *sums] + sq
            ring[1, *sums] = pr if k == 0 else ring[1, *sums] + pr

        def r_tiles(lo, hi):
            for k in range(lo, hi + 1):
                if k > lo:
                    r_done(k - 1)
                if k < hi:
                    gp[:, cols(k)] = lax.dot_general(ub[1], w1[cols(k), :], LAST_DIMS, preferred_element_type=F32)

        r_tiles(0, d_half)
        u_out(1, rows).wait()
        load_gp(nxt, lo=d)

        @pl.when(early)
        def _():
            prefetch(nxt, step + 1, before)

        r_tiles(d_half, d_tiles)
        keep = idx < N_OWN
        part_rows = ROWS // 4
        for h in range(4):
            rws = pl.ds(h * part_rows, part_rows)
            q = lax.rsqrt(jnp.sum(ring[0, rws, pl.ds(0, 128)], axis=-1, keepdims=True) * (1.0 / d) + EPS)
            mean = q * jnp.sum(ring[1, rws, pl.ds(0, 128)], axis=-1, keepdims=True) * (1.0 / d)
            qqm = q * q * mean
            for k in range(d // 128):
                lanes = pl.ds(k * 128, 128)
                xk = rb[1, rws, lanes].astype(F32)
                drk = gp[rws, lanes]
                dhk = main[slot, rws, lanes].astype(F32)
                main[slot, rws, lanes] = (dhk + (q * (drk * gain[:, lanes]) - xk * qqm)).astype(BF16)
                part = jnp.sum((drk * (xk * q)).reshape(part_rows // 8, 8, 128), axis=0)
                dgp[:, lanes] += jnp.where(keep, part, 0.0)

        @pl.when(sid > 0)
        def _():
            remote(main.at[slot], dh_all.at[rows, :], slot_snd.at[slot], dh_rcv.at[idx],
                   stage=jnp.maximum(sid - 1, 0)).start()

        load_gp(nxt, hi=d)

        @pl.when(idx == N_CHAIN - 1)
        def _():
            remote(dgp, dgr, dg_snd, dg_rcv, data=other).start()

            @pl.when(last)
            def _():
                red = lossacc[:, pl.ds(0, 128)]
                for k in range(1, d // 128):
                    red = red + lossacc[:, pl.ds(k * 128, 128)]
                lossred[...] = red
                for hop in range(1, 4):
                    remote(lossred, lossbuf.at[me_y], loss_snd.at[hop - 1], loss_rcv.at[me_y], stage=3 - hop).start()
                for hop in range(4):
                    remote(lossred, lossbuf.at[me_y], loss_snd.at[3 + hop], loss_rcv.at[me_y],
                           data=other, stage=3 - hop).start()

    def finish(b3, b2, b1):
        @pl.when(fields(b1)[0] == AUX)
        def _():
            u_out(1, pl.ds(0, ROWS)).wait()

        for back, code in ((3, b3), (2, b2), (1, b1)):
            wait_slot_send(code, (n_items - back) % 3)

        def end_relays(k, carry):
            relay_r(k).wait_send()
            relay_dh(k).wait_send()
            return carry

        lax.fori_loop(0, N_EXCH, end_relays, 0)

        @pl.when(first)
        def _():
            share_x.wait_send()

        @pl.when(last)
        def _():
            share_y.wait_send()

        dg_copy = remote(dgp, dgr, dg_snd, dg_rcv, data=other)
        dg_copy.wait_send()
        dg_copy.wait_recv()
        dg_out[...] = jnp.sum(dgp[...] + dgr[...], axis=0, keepdims=True)

        @pl.when(last)
        def _():
            for hop in range(7):
                remote(lossred, lossbuf.at[me_y], loss_snd.at[hop], loss_rcv.at[me_y], data=other).wait_send()
            lossbuf[me_y] = lossred[...]

        @pl.when(jnp.logical_not(last))
        def _():
            local(lossred, lossbuf.at[me_y], loss_rcv.at[me_y]).wait()

        local(lossred, lossbuf.at[other], loss_rcv.at[other]).wait()
        loss_out[0] = jnp.sum(lossbuf[0] + lossbuf[1]) / (tok_total * d)

    def item(step, carry):
        b3, b2, b1, cur = carry
        nxt = decode(step + 1)
        kind, idx, ready = fields(cur)
        slot = lax.rem(step, 3)
        early = fields(nxt)[2] & (step + 1 < n_items)
        after_aux = fields(b1)[0] == AUX
        rows = rows_of(jnp.where(kind == AUX, other * N_OWN + idx, own_chunk(idx)))

        @pl.when(step == n_items)
        def _():
            finish(b3, b2, b1)

        @pl.when(jnp.logical_not(ready))
        def _():
            prefetch(cur, step, b3)

        @pl.when(kind == PRE)
        def _():
            run_pre(step, idx, slot, nxt, early, b2, b1)

        @pl.when((kind == FWD) | (kind == AUX))
        def _():
            up_phase(step, kind, idx, slot, rows)

        @pl.when(kind == FWD)
        def _():
            down_phase(step, idx, slot, nxt, early, b2, after_aux)

        @pl.when((kind == BWD) | (kind == AUX))
        def _():
            back_phase(step, kind, idx, slot, rows, nxt, early, b2, after_aux)

        @pl.when(kind == BWD)
        def _():
            grad_phase(step, idx, slot, rows, nxt, early, b2)

        return b2, b1, cur, nxt

    none = jnp.int32(NONE)
    lax.fori_loop(0, n_items + 1, item, (none, none, none, decode(0)))


def grads_kernel(r_all, u_all, da_all, dh_all, d_up, d_down, pool, outs, held_ld, ring_ld, out_st):
    n_stream, n_held = u_all.shape[1] // TILE, dh_all.shape[1] // TILE
    n_ring = 3
    cols = lambda k: pl.ds(pl.multiple_of(k * TILE, TILE), TILE)

    def load_held(phase, j):
        src = dh_all if phase == 0 else r_all
        return pltpu.make_async_copy(src.at[:, cols(j)], pool.at[n_ring + phase * n_held + j], held_ld.at[phase, j])

    def load_ring(phase, k, slot):
        src = u_all if phase == 0 else da_all
        return pltpu.make_async_copy(src.at[:, cols(k)], pool.at[slot], ring_ld.at[slot])

    def store(phase, k, j, half):
        dst = d_down.at[cols(k), cols(j)] if phase == 0 else d_up.at[cols(j), cols(k)]
        return pltpu.make_async_copy(outs.at[half, j], dst, out_st.at[half, j])

    def body(count, carry):
        second = count >= n_stream
        k = lax.rem(count, n_stream)
        slot, half = lax.rem(count, n_ring), lax.rem(count, 2)
        load_ring(0, 0, slot).wait()
        ahead, next_k = lax.rem(count + 2, n_ring), lax.rem(count + 2, n_stream)

        @pl.when(count + 2 < n_stream)
        def _():
            load_ring(0, next_k, ahead).start()

        @pl.when((count + 2 >= n_stream) & (count + 2 < 2 * n_stream))
        def _():
            load_ring(1, next_k, ahead).start()

        for phase, at in ((0, 0), (1, n_stream)):
            @pl.when(count == at)
            def _():
                for j in range(n_held):
                    load_held(phase, j).wait()

        @pl.when(count == 1)
        def _():
            for j in range(n_held):
                load_held(1, j).start()

        @pl.when(count >= 2)
        def _():
            for j in range(n_held):
                store(0, 0, j, half).wait()

        for j in range(n_held):
            left = jnp.where(second, n_ring + n_held + j, slot)
            right = jnp.where(second, slot, n_ring + j)
            outs[half, j] = lax.dot_general(pool[left], pool[right], ROW_DIMS, preferred_element_type=F32)

        for phase in range(2):
            @pl.when(second if phase else jnp.logical_not(second))
            def _():
                for j in range(n_held):
                    store(phase, k, j, half).start()

        return carry

    load_ring(0, 0, 0).start()
    for j in range(n_held):
        load_held(0, j).start()
    load_ring(0, 1, 1).start()
    lax.fori_loop(0, 2 * n_stream, body, 0)
    for half in range(2):
        for j in range(n_held):
            store(0, 0, j, half).wait()


def encode(order):
    return tuple("FBAP".index(name[0]) + 4 * int(name[1:].rstrip("~")) + 64 * int(not name.endswith("~")) for name in order)


def solution(mesh):
    n_data = mesh.shape["data"]
    orders = tuple(encode(order) for order in ORDERS)

    def local_step(x_in, y_tgt, w_up, w_down, gain):
        n_micro, tokens, d = x_in.shape
        ff = w_up.shape[2]
        own = n_micro * tokens
        total = n_data * own
        x_rows, y_rows = x_in.reshape(own, d), y_tgt.reshape(own, d)
        hbm = pl.BlockSpec(memory_space=pl.ANY)
        vmem = pl.BlockSpec(memory_space=pltpu.VMEM)
        dma, sem = pltpu.SemaphoreType.DMA, pltpu.SemaphoreType.DMA(())
        out = pl.pallas_call(
            functools.partial(chain_kernel, orders, total),
            out_shape=(
                jax.ShapeDtypeStruct((total, d), BF16),
                jax.ShapeDtypeStruct((total, ff), BF16),
                jax.ShapeDtypeStruct((total, ff), BF16),
                jax.ShapeDtypeStruct((total, d), BF16),
                jax.ShapeDtypeStruct((N_CHAIN * ROWS, ff), F32),
                jax.ShapeDtypeStruct((N_CHAIN * ROWS, d), BF16),
                jax.ShapeDtypeStruct((ROWS, d), BF16),
                jax.ShapeDtypeStruct((1, d), F32),
                jax.ShapeDtypeStruct((1,), F32),
            ),
            in_specs=[hbm, hbm, hbm, hbm, vmem],
            out_specs=[hbm] * 7 + [vmem, pl.BlockSpec(memory_space=pltpu.SMEM)],
            scratch_shapes=[
                pltpu.VMEM((d, ff), BF16),
                pltpu.VMEM((ff, d), BF16),
                pltpu.VMEM((3, ROWS, d), BF16),
                pltpu.VMEM((2, ROWS, d), BF16),
                pltpu.VMEM((ROWS, ff), F32),
                pltpu.VMEM((2, ROWS, ff), BF16),
                pltpu.VMEM((2, ROWS, TILE), F32),
                pltpu.VMEM((8, d), F32),
                pltpu.VMEM((8, d), F32),
                pltpu.VMEM((8, d), F32),
                pltpu.VMEM((8, 128), F32),
                pltpu.VMEM((2, 8, 128), F32),
                dma((3,)), dma((3,)), dma((2,)), sem, sem, sem, dma((2,)), sem,
                dma((N_CHAIN + N_PRE,)), dma((N_CHAIN,)), dma((N_EXCH,)), dma((N_EXCH,)), sem, sem, dma((2,)),
                dma((3,)), dma((N_EXCH,)), dma((N_EXCH,)), sem, sem, dma((7,)),
            ],
            compiler_params=pltpu.CompilerParams(has_side_effects=True, vmem_limit_bytes=67043328),
            name="chain",
        )(x_rows, y_rows, w_up[0], w_down[0], gain)
        r_all, u_all, da_all, dh_all = out[:4]
        n_held = d // TILE
        d_up, d_down = pl.pallas_call(
            grads_kernel,
            out_shape=(jax.ShapeDtypeStruct((d, ff), F32), jax.ShapeDtypeStruct((ff, d), F32)),
            in_specs=[hbm] * 4,
            out_specs=[hbm] * 2,
            scratch_shapes=[
                pltpu.VMEM((3 + 2 * n_held, total, TILE), BF16),
                pltpu.VMEM((2, n_held, TILE, TILE), F32),
                dma((2, n_held)), dma((3,)), dma((2, n_held)),
            ],
            compiler_params=pltpu.CompilerParams(vmem_limit_bytes=67043328),
            name="grads",
        )(r_all, u_all, da_all, dh_all)
        return d_up[None], d_down[None], out[7], out[8]

    return jax.shard_map(local_step, mesh=mesh, in_specs=(P(("part", "data"), None, None), P(("part", "data"), None, None), P("stage", None, None), P("stage", None, None), P("stage", None)), out_specs=(P(("part", "stage"), None, None), P(("part", "stage"), None, None), P(("part", "stage"), None), P("part")), check_vma=False)
```

profile of v0, /device:TPU:0, one launch (start us, length us, event | category | flops | bytes accessed | tf_op | source)
XLA Modules:
  0.0 627.0 jit_solution(4369209333473543192)
XLA Ops:
  0.6 418.9 %chain.1 = (bf16[4096,2048]{1,0:T(8,128)(2,1)}, bf16[4096,5632]{1,0:T(8,128)(2,1)}, bf16[4096,5632]{1,0:T(8,128)(2,1)}, bf16[4096,2048]{1,0:T(8,128)(2,1)}, f32[...) custom-call(bf16[2048,2048]{1,0:T(8,128)(2,1)} %bitcast.8, ...), custom_call_target="tpu_custom_call" | custom-call | tf_op jit(solution)/shard_map/chain/pallas_call | solution.py:710
  419.6 204.3 %grads.1 = (f32[2048,5632]{1,0:T(8,128)}, f32[5632,2048]{1,0:T(8,128)}) custom-call(bf16[4096,2048]{1,0:T(8,128)(2,1)} %get-tuple-element.12.r_all, bf16[4096,5632]{1,0:T(8,128)(2,1)} %get-tuple-element.13.u_all, bf16[4096,5632]{1,0:T(8,128)(2,1)} %get-tuple-element.14.da_all, bf16[4096,2048]{1,0:T(8,128)(2,1)} %get-tuple-element.15.dh_all), custom_call_target="tpu_custom_call" | custom-call | tf_op jit(solution)/shard_map/grads/pallas_call | solution.py:747
  623.9 1.3 copy.11
where the time goes:
time: 627 us
  Pallas kernels  623 us (99%)
    pallas_call x1, Pallas kernels, local_step(): pl.pallas_call(functools.partial(chain_kernel, orders, total), out_shape=...  419 us
    pallas_call x1, Pallas kernels, local_step(): pl.pallas_call(grads_kernel, out_shape=(jax.ShapeDtypeStruct((d, ff), F32...  204 us

commit v1 on v0

--- a/solution.py
+++ b/solution.py
@@ -24,13 +24,13 @@
 ORDERS = (
     (
         "P0~", "P1", "P2", "P3", "F2", "F3", "F4", "F5", "F6",
-        "F7", "F8", "B0~", "B1~", "B2~", "A0", "A1", "A2~", "B3",
-        "B4", "A3", "A4", "B5", "B6", "A5", "A6", "B7", "B8",
+        "F7", "B0~", "F8", "B1~", "A0", "A1", "B2~", "A2~", "B3",
+        "B4", "A3~", "B5", "A4", "B6", "A5", "A6", "B7", "B8",
     ),
     (
-        "P0~", "P1~", "P2", "P3", "F2~", "F3~", "F4~", "F5", "B0",
-        "F6", "F7", "B1", "B2~", "A0", "F8", "B3", "B4~", "A1",
-        "A2", "B5", "B6~", "A3", "A4", "B7~", "B8", "A5", "A6",
+        "P0~", "P1~", "P2", "P3", "F2~", "F3~", "F4~", "B0~", "F5",
+        "F6", "B1~", "A0", "F7", "B2", "F8", "B3", "B4~", "A1",
+        "B5~", "A2", "B6", "A3", "A4", "B7", "B8", "A5", "A6",
     ),
     (
         "P0~", "P1~", "P2~", "P3~", "B0~", "F2", "F3", "B1", "F4",
@@ -47,6 +47,7 @@
 N_OWN = 8
 N_EXCH = 7
 N_PRE = 2
+N_AHEAD = 4
 
 
 def gelu_and_grad(pre):
@@ -175,6 +176,10 @@
             def _():
                 relay_dh(idx).start()
 
+            @pl.when((sid < 2) & (idx < N_EXCH - N_AHEAD))
+            def _():
+                relay_r(jnp.minimum(idx + N_AHEAD, N_EXCH - 1)).start()
+
         @pl.when(kind == AUX)
         def _():
             rows = rows_of(other * N_OWN + idx)
@@ -195,7 +200,9 @@
 
         @pl.when((kind == BWD) & jnp.logical_not(last))
         def _():
-            local(gp_all.at[rows_of(idx), lanes], gp.at[:, lanes], gp_i).start()
+            for k in range(4):
+                quarter = pl.ds(pl.multiple_of(idx * ROWS + k * (ROWS // 4), ROWS // 4), ROWS // 4)
+                local(gp_all.at[quarter, lanes], gp.at[pl.ds(k * (ROWS // 4), ROWS // 4), lanes], gp_i).start()
 
     def normalise(slot, rws):
         acc = jnp.zeros((rws.size, 128), F32)
@@ -218,15 +225,22 @@
                 ring[k % 2, pl.ds(0, n), :] = jnp.dot(rb[0, rws, :], w1[:, cols(k)], preferred_element_type=F32)
 
     def down_tiles(lo, hi, slot, out_slot, rws, count):
-        n = rws.size
+        n, slab = rws.size, HALF // 2
+
+        def done(k):
+            for r in range(n // slab):
+                at = rws.start + r * slab
+                rw = pl.ds(at if isinstance(at, int) else pl.multiple_of(at, slab), slab)
+                upd = ring[k % 2, pl.ds(r * slab, slab), :]
+                h = (main[slot, rw, cols(k)].astype(F32) + upd).astype(BF16)
+                err = h.astype(F32) - rb[1, rw, cols(k)].astype(F32)
+                main[out_slot, rw, cols(k)] = jnp.where(last, (err * (1.0 / tok_total)).astype(BF16), h)
+                part = jnp.sum((err * err).reshape(slab // 8, 8, TILE), axis=0)
+                lossacc[:, cols(k)] += jnp.where(count, part, 0.0)
+
         for k in range(lo, hi + 1):
             if k > lo:
-                upd = ring[(k - 1) % 2, pl.ds(0, n), :]
-                h = (main[slot, rws, cols(k - 1)].astype(F32) + upd).astype(BF16)
-                err = h.astype(F32) - rb[1, rws, cols(k - 1)].astype(F32)
-                main[out_slot, rws, cols(k - 1)] = jnp.where(last, (err * (1.0 / tok_total)).astype(BF16), h)
-                part = jnp.sum((err * err).reshape(n // 8, 8, TILE), axis=0)
-                lossacc[:, cols(k - 1)] += jnp.where(count, part, 0.0)
+                done(k - 1)
             if k < hi:
                 ring[k % 2, pl.ds(0, n), :] = jnp.dot(ub[0, rws, :], w2[:, cols(k)], preferred_element_type=F32)
 
@@ -247,6 +261,13 @@
         for k in range(2):
             load_w2(k).start()
 
+    barrier = pltpu.get_barrier_semaphore()
+    for far in range(2):
+        for hop in range(int(far == 0), 4):
+            pl.semaphore_signal(barrier, inc=1, device_id={"data": other if far else me_y, "stage": lax.rem(sid + hop, 4)},
+                                device_id_type=MESH)
+    pl.semaphore_wait(barrier, 7)
+
     share = pl.ds(N_EXCH * ROWS, ROWS)
     share_x = remote(x_in.at[share, :], x_land.at[pl.ds(N_OWN * ROWS, ROWS), :], red_snd, x_rcv.at[N_OWN], data=other)
     share_y = remote(y_tgt.at[share, :], y_land, red_snd, y_rcv, data=other)
@@ -382,7 +403,7 @@
         def _():
             r_out.wait()
 
-        @pl.when(fwd & (idx < N_EXCH))
+        @pl.when(fwd & (idx < jnp.where(sid < 2, N_AHEAD, N_EXCH)))
         def _():
             relay_r(jnp.minimum(idx, N_EXCH - 1)).start()
 
@@ -466,19 +487,39 @@
             relay_dh(jnp.minimum(idx, N_EXCH - 1)).start()
 
     def grad_phase(step, idx, slot, rows, nxt, early, before):
+        load_gp(nxt, lo=d)
+
+        @pl.when(early)
+        def _():
+            prefetch(nxt, step + 1, before)
+
         local(x_land.at[pl.ds(0, ROWS), :], rb.at[1], rb_ld.at[1]).wait()
 
+        sums = pl.ds(0, 128)
+        keep = jnp.where(idx < N_OWN, 0, 1)
+        part_rows = ROWS // 4
+
+        def inv_rms():
+            for h in range(4):
+                rws = pl.ds(h * part_rows, part_rows)
+                acc = jnp.zeros((part_rows, 128), F32)
+                for k in range(d // 128):
+                    xk = rb[1, rws, pl.ds(k * 128, 128)].astype(F32)
+                    acc = acc + xk * xk
+                q = lax.rsqrt(jnp.sum(acc, axis=-1, keepdims=True) * (1.0 / d) + EPS)
+                ring[0, rws, sums] = jnp.broadcast_to(q, (part_rows, 128))
+
         def r_done(k):
-            sq = jnp.zeros((ROWS, 128), F32)
-            pr = jnp.zeros((ROWS, 128), F32)
-            for j in range(TILE // 128):
-                lanes = pl.ds(k * TILE + j * 128, 128)
-                xk = rb[1, :, lanes].astype(F32)
-                sq = sq + xk * xk
-                pr = pr + gp[:, lanes] * gain[:, lanes] * xk
-            sums = (pl.ds(0, ROWS), pl.ds(0, 128))
-            ring[0, *sums] = sq if k == 0 else ring[0, *sums] + sq
-            ring[1, *sums] = pr if k == 0 else ring[1, *sums] + pr
+            for h in range(4):
+                rws = pl.ds(h * part_rows, part_rows)
+                pr = jnp.zeros((part_rows, 128), F32)
+                for j in range(TILE // 128):
+                    lanes = pl.ds(k * TILE + j * 128, 128)
+                    unit = rb[1, rws, lanes].astype(F32) * ring[0, rws, sums]
+                    prod = gp[rws, lanes] * unit
+                    pr = pr + prod * gain[:, lanes]
+                    dgp[keep, :, lanes] += jnp.sum(prod.reshape(part_rows // 8, 8, 128), axis=0)
+                ring[1, rws, sums] = pr if k == 0 else ring[1, rws, sums] + pr
 
         def r_tiles(lo, hi):
             for k in range(lo, hi + 1):
@@ -486,31 +527,18 @@
                     r_done(k - 1)
                 if k < hi:
                     gp[:, cols(k)] = lax.dot_general(ub[1], w1[cols(k), :], LAST_DIMS, preferred_element_type=F32)
-
-        r_tiles(0, d_half)
-        u_out(1, rows).wait()
-        load_gp(nxt, lo=d)
-
-        @pl.when(early)
-        def _():
-            prefetch(nxt, step + 1, before)
-
-        r_tiles(d_half, d_tiles)
-        keep = idx < N_OWN
-        part_rows = ROWS // 4
+                if k == 0:
+                    inv_rms()
+
+        r_tiles(0, d_tiles)
         for h in range(4):
             rws = pl.ds(h * part_rows, part_rows)
-            q = lax.rsqrt(jnp.sum(ring[0, rws, pl.ds(0, 128)], axis=-1, keepdims=True) * (1.0 / d) + EPS)
-            mean = q * jnp.sum(ring[1, rws, pl.ds(0, 128)], axis=-1, keepdims=True) * (1.0 / d)
-            qqm = q * q * mean
+            q = ring[0, rws, sums]
+            q_mean = q * (jnp.sum(ring[1, rws, sums], axis=-1, keepdims=True) * (1.0 / d))
             for k in range(d // 128):
                 lanes = pl.ds(k * 128, 128)
-                xk = rb[1, rws, lanes].astype(F32)
-                drk = gp[rws, lanes]
-                dhk = main[slot, rws, lanes].astype(F32)
-                main[slot, rws, lanes] = (dhk + (q * (drk * gain[:, lanes]) - xk * qqm)).astype(BF16)
-                part = jnp.sum((drk * (xk * q)).reshape(part_rows // 8, 8, 128), axis=0)
-                dgp[:, lanes] += jnp.where(keep, part, 0.0)
+                dx = q * (gp[rws, lanes] * gain[:, lanes] - rb[1, rws, lanes].astype(F32) * q_mean)
+                main[slot, rws, lanes] = (main[slot, rws, lanes].astype(F32) + dx).astype(BF16)
 
         @pl.when(sid > 0)
         def _():
@@ -518,10 +546,11 @@
                    stage=jnp.maximum(sid - 1, 0)).start()
 
         load_gp(nxt, hi=d)
-
-        @pl.when(idx == N_CHAIN - 1)
-        def _():
-            remote(dgp, dgr, dg_snd, dg_rcv, data=other).start()
+        u_out(1, rows).wait()
+
+        @pl.when(idx == N_OWN - 1)
+        def _():
+            remote(dgp.at[0], dgr, dg_snd, dg_rcv, data=other).start()
 
             @pl.when(last)
             def _():
@@ -558,10 +587,10 @@
         def _():
             share_y.wait_send()
 
-        dg_copy = remote(dgp, dgr, dg_snd, dg_rcv, data=other)
+        dg_copy = remote(dgp.at[0], dgr, dg_snd, dg_rcv, data=other)
         dg_copy.wait_send()
         dg_copy.wait_recv()
-        dg_out[...] = jnp.sum(dgp[...] + dgr[...], axis=0, keepdims=True)
+        dg_out[...] = jnp.sum(dgp[0] + dgr[...], axis=0, keepdims=True)
 
         @pl.when(last)
         def _():
@@ -619,7 +648,7 @@
     lax.fori_loop(0, n_items + 1, item, (none, none, none, decode(0)))
 
 
-def grads_kernel(r_all, u_all, da_all, dh_all, d_up, d_down, pool, outs, held_ld, ring_ld, out_st):
+def grads_kernel(r_all, u_all, da_all, dh_all, dg, loss, d_up, d_down, dg_out, loss_out, pool, outs, held_ld, ring_ld, out_st, small):
     n_stream, n_held = u_all.shape[1] // TILE, dh_all.shape[1] // TILE
     n_ring = 3
     cols = lambda k: pl.ds(pl.multiple_of(k * TILE, TILE), TILE)
@@ -684,7 +713,13 @@
     for j in range(n_held):
         load_held(0, j).start()
     load_ring(0, 1, 1).start()
+    pass_dg = pltpu.make_async_copy(dg, dg_out, small.at[0])
+    pass_loss = pltpu.make_async_copy(loss, loss_out, small.at[1])
+    pass_dg.start()
+    pass_loss.start()
     lax.fori_loop(0, 2 * n_stream, body, 0)
+    pass_dg.wait()
+    pass_loss.wait()
     for half in range(2):
         for j in range(n_held):
             store(0, 0, j, half).wait()
@@ -730,7 +765,7 @@
                 pltpu.VMEM((ROWS, ff), F32),
                 pltpu.VMEM((2, ROWS, ff), BF16),
                 pltpu.VMEM((2, ROWS, TILE), F32),
-                pltpu.VMEM((8, d), F32),
+                pltpu.VMEM((2, 8, d), F32),
                 pltpu.VMEM((8, d), F32),
                 pltpu.VMEM((8, d), F32),
                 pltpu.VMEM((8, 128), F32),
@@ -739,24 +774,28 @@
                 dma((N_CHAIN + N_PRE,)), dma((N_CHAIN,)), dma((N_EXCH,)), dma((N_EXCH,)), sem, sem, dma((2,)),
                 dma((3,)), dma((N_EXCH,)), dma((N_EXCH,)), sem, sem, dma((7,)),
             ],
-            compiler_params=pltpu.CompilerParams(has_side_effects=True, vmem_limit_bytes=67043328),
+            compiler_params=pltpu.CompilerParams(collective_id=0, has_side_effects=True, vmem_limit_bytes=67043328),
             name="chain",
         )(x_rows, y_rows, w_up[0], w_down[0], gain)
-        r_all, u_all, da_all, dh_all = out[:4]
         n_held = d // TILE
-        d_up, d_down = pl.pallas_call(
+        d_up, d_down, d_gain, loss = pl.pallas_call(
             grads_kernel,
-            out_shape=(jax.ShapeDtypeStruct((d, ff), F32), jax.ShapeDtypeStruct((ff, d), F32)),
-            in_specs=[hbm] * 4,
-            out_specs=[hbm] * 2,
+            out_shape=(
+                jax.ShapeDtypeStruct((d, ff), F32),
+                jax.ShapeDtypeStruct((ff, d), F32),
+                jax.ShapeDtypeStruct((1, d), F32),
+                jax.ShapeDtypeStruct((1,), F32),
+            ),
+            in_specs=[hbm] * 6,
+            out_specs=[hbm] * 4,
             scratch_shapes=[
                 pltpu.VMEM((3 + 2 * n_held, total, TILE), BF16),
                 pltpu.VMEM((2, n_held, TILE, TILE), F32),
-                dma((2, n_held)), dma((3,)), dma((2, n_held)),
+                dma((2, n_held)), dma((3,)), dma((2, n_held)), dma((2,)),
             ],
             compiler_params=pltpu.CompilerParams(vmem_limit_bytes=67043328),
             name="grads",
-        )(r_all, u_all, da_all, dh_all)
-        return d_up[None], d_down[None], out[7], out[8]
+        )(*out[:4], *out[7:])
+        return d_up[None], d_down[None], d_gain, loss
 
     return jax.shard_map(local_step, mesh=mesh, in_specs=(P(("part", "data"), None, None), P(("part", "data"), None, None), P("stage", None, None), P("stage", None, None), P("stage", None)), out_specs=(P(("part", "stage"), None, None), P(("part", "stage"), None, None), P(("part", "stage"), None), P("part")), check_vma=False)

time: 627 us -> 611 us (0.974)
  Pallas kernels: 623 us -> 610 us
    pallas_call x1, Pallas kernels: 419 us -> 405 us  [local_step(): pl.pallas_call(functools.partial(chain_kernel, orders, total), out_shape=...]
where the time goes in v1:
time: 611 us
  Pallas kernels  610 us (100%)
    pallas_call x1, Pallas kernels, local_step(): pl.pallas_call(functools.partial(chain_kernel, orders, total), out_shape=...  405 us
    pallas_call x1, Pallas kernels, local_step(): pl.pallas_call(grads_kernel, out_shape=(jax.ShapeDtypeStruct((d, ff), F32...  205 us

profile of v1, /device:TPU:0, one launch (start us, length us, event | category | flops | bytes accessed | tf_op | source)
XLA Modules:
  0.0 610.9 jit_solution(6058967024101109579)
XLA Ops:
  0.6 405.1 %chain.1 = (bf16[4096,2048]{1,0:T(8,128)(2,1)}, bf16[4096,5632]{1,0:T(8,128)(2,1)}, bf16[4096,5632]{1,0:T(8,128)(2,1)}, bf16[4096,2048]{1,0:T(8,128)(2,1)}, f32[...) custom-call(bf16[2048,2048]{1,0:T(8,128)(2,1)} %bitcast.8, ...), custom_call_target="tpu_custom_call" | custom-call | tf_op jit(solution)/shard_map/chain/pallas_call | solution.py:745
  405.8 205.0 %grads.1 = (f32[2048,5632]{1,0:T(8,128)}, f32[5632,2048]{1,0:T(8,128)}, f32[1,2048]{1,0:T(1,128)}, f32[1]{0:T(128)}) custom-call(bf16[4096,2048]{1,0:T(8,128)(2,1)} %get-tuple-element.14.r_all, bf16[4096,5632]{1,0:T(8,128)(2,1)} %get-tuple-element.15.u_all, bf16[4096,5632]{1,0:T(8,128)(2,1)} %get-tuple-element.16.da_all, ...), custom_call_target="tpu_custom_call" | custom-call | tf_op jit(solution)/shard_map/grads/pallas_call | solution.py:781

commit v2 on v1

--- a/solution.py
+++ b/solution.py
@@ -531,17 +531,17 @@
                     inv_rms()
 
         r_tiles(0, d_tiles)
-        for h in range(4):
-            rws = pl.ds(h * part_rows, part_rows)
-            q = ring[0, rws, sums]
-            q_mean = q * (jnp.sum(ring[1, rws, sums], axis=-1, keepdims=True) * (1.0 / d))
-            for k in range(d // 128):
-                lanes = pl.ds(k * 128, 128)
-                dx = q * (gp[rws, lanes] * gain[:, lanes] - rb[1, rws, lanes].astype(F32) * q_mean)
-                main[slot, rws, lanes] = (main[slot, rws, lanes].astype(F32) + dx).astype(BF16)
-
         @pl.when(sid > 0)
         def _():
+            for h in range(4):
+                rws = pl.ds(h * part_rows, part_rows)
+                q = ring[0, rws, sums]
+                q_mean = q * (jnp.sum(ring[1, rws, sums], axis=-1, keepdims=True) * (1.0 / d))
+                for k in range(d // 128):
+                    lanes = pl.ds(k * 128, 128)
+                    dx = q * (gp[rws, lanes] * gain[:, lanes] - rb[1, rws, lanes].astype(F32) * q_mean)
+                    main[slot, rws, lanes] = (main[slot, rws, lanes].astype(F32) + dx).astype(BF16)
+
             remote(main.at[slot], dh_all.at[rows, :], slot_snd.at[slot], dh_rcv.at[idx],
                    stage=jnp.maximum(sid - 1, 0)).start()
 

time: 611 us -> 608 us (level)
  no operation moved by 1% of the time
where the time goes in v2:
time: 608 us
  Pallas kernels  607 us (100%)
    pallas_call x1, Pallas kernels, local_step(): pl.pallas_call(functools.partial(chain_kernel, orders, total), out_shape=...  402 us
    pallas_call x1, Pallas kernels, local_step(): pl.pallas_call(grads_kernel, out_shape=(jax.ShapeDtypeStruct((d, ff), F32...  205 us

profile of v2, /device:TPU:0, one launch (start us, length us, event | category | flops | bytes accessed | tf_op | source)
XLA Modules:
  0.0 607.9 jit_solution(12135833391111263756)
XLA Ops:
  0.6 402.0 %chain.1 = (bf16[4096,2048]{1,0:T(8,128)(2,1)}, bf16[4096,5632]{1,0:T(8,128)(2,1)}, bf16[4096,5632]{1,0:T(8,128)(2,1)}, bf16[4096,2048]{1,0:T(8,128)(2,1)}, f32[...) custom-call(bf16[2048,2048]{1,0:T(8,128)(2,1)} %bitcast.8, ...), custom_call_target="tpu_custom_call" | custom-call | tf_op jit(solution)/shard_map/chain/pallas_call | solution.py:745
  402.7 205.0 %grads.1 = (f32[2048,5632]{1,0:T(8,128)}, f32[5632,2048]{1,0:T(8,128)}, f32[1,2048]{1,0:T(1,128)}, f32[1]{0:T(128)}) custom-call(bf16[4096,2048]{1,0:T(8,128)(2,1)} %get-tuple-element.14.r_all, bf16[4096,5632]{1,0:T(8,128)(2,1)} %get-tuple-element.15.u_all, bf16[4096,5632]{1,0:T(8,128)(2,1)} %get-tuple-element.16.da_all, ...), custom_call_target="tpu_custom_call" | custom-call | tf_op jit(solution)/shard_map/grads/pallas_call | solution.py:781
